TPU v7x, 32 devices: a whole 2x2x4 slice. The times are simulated.
32 devices in a mesh: row: 4 (over x, core), col: 8 (over z, y).
Axes of the slice: x: 2, y: 2, z: 4, core: 2. Of those that a mesh axis runs over, the one named last changes fastest.
Arguments:
- rows: bfloat16 [1024, 4096], P(('row', 'col')), may hold values from -6 to 6
- task_ids: int32 [1024], P(('row', 'col')), may hold values from 0 to 8, as said below
- task_embed: bfloat16 [8, 4096], replicated, may hold values from -6 to 6
- norm_gain: float32 [4, 4096], replicated, may hold values from 0.1 to 1.9
- layer_weight: bfloat16 [4, 4096, 4096], P(None, None, 'col'), may hold values from -0.09375 to 0.09375
Outputs:
- packed_out: bfloat16 [1024, 4096], P('row', 'col')
Inputs may be any that keep to these rules, and one draw needn't show every extreme that they name: `task_ids`: 8 marks an empty row, smaller values name a task.
All inputs are finite; a program needn't handle non-finite values.
Results may differ from a plain program's by a relative error of at most 0.008.
Values may be sent and summed in bfloat16 or wider, within the bound.
A program may use at most 128 MiB of HBM per device.

v0:
```python
import jax
import jax.numpy as jnp
from jax import lax
from jax.sharding import PartitionSpec as P

epsilon = 1e-06


def entering(part, axis, combine, identity):
    place = lax.axis_index(axis)
    gathered = lax.all_gather(part, axis)
    state = jnp.zeros_like(part) + jnp.asarray(identity, part.dtype)

    def one(hop, state):
        return combine(state, lax.dynamic_index_in_dim(gathered, hop, 0, False))

    return lax.fori_loop(0, place, one, state)


def add_counts(earlier, later):
    return earlier + later


def activate_rows(hidden, gain):
    total_rows = hidden.shape[0]
    width = hidden.shape[1]
    block_rows = min(512, total_rows)

    def one_block(block):
        values = block.astype(jnp.float32)
        inverse_rms = lax.rsqrt(jnp.mean(values * values, axis=1, keepdims=True) + epsilon)
        return jax.nn.silu(values * inverse_rms * gain[None, :]).astype(jnp.bfloat16)

    blocks = hidden.reshape(total_rows // block_rows, block_rows, width)
    return lax.map(one_block, blocks).reshape(total_rows, width)


def shards(rows, task_ids, task_embed, norm_gain, layer_weight):
    row_count = rows.shape[0]
    width = rows.shape[1]
    task_count = task_embed.shape[0]
    row_devices = lax.axis_size("row")
    col_devices = lax.axis_size("col")
    capacity = row_count // row_devices + task_count
    slots_group = row_count * col_devices
    task_range = jnp.arange(task_count, dtype=jnp.int32)
    member = (task_ids[:, None] == task_range[None, :]).astype(jnp.int32)
    counts = jnp.sum(member, axis=0)
    zero_counts = jnp.zeros_like(counts)
    before_col = entering(counts, "col", add_counts, zero_counts)
    row_total = lax.psum(counts, "col")
    before_row = entering(row_total, "row", add_counts, zero_counts)
    totals = lax.psum(row_total, "row")
    before = before_row + before_col
    task_base = jnp.cumsum(totals) - totals
    positions = jnp.arange(row_count, dtype=jnp.int32)
    earlier_mask = positions[None, :] < positions[:, None]
    same_task = task_ids[:, None] == task_ids[None, :]
    task_rank = jnp.sum((same_task & earlier_mask).astype(jnp.int32), axis=1)
    row_live = task_ids < task_count
    packed_pos = (
        jnp.sum(member * (task_base + before)[None, :], axis=1).astype(jnp.int32) + task_rank
    )
    target_row = packed_pos % row_devices
    slot_index = packed_pos // row_devices
    before_pos = packed_pos[None, :] < packed_pos[:, None]
    same_target = (target_row[:, None] == target_row[None, :]) & row_live[None, :]
    within = jnp.sum((same_target & before_pos).astype(jnp.int32), axis=1)
    send_at = jnp.where(row_live, target_row * capacity + within, -1)
    buffer_range = jnp.arange(row_devices * capacity, dtype=jnp.int32)
    select = buffer_range[:, None] == send_at[None, :]
    send_rows = jnp.dot(
        select.astype(jnp.bfloat16), rows, preferred_element_type=jnp.float32
    ).astype(jnp.bfloat16)
    send_rows = send_rows.reshape(row_devices, capacity, width)
    send_slots = jnp.sum(jnp.where(select, slot_index[None, :] + 1, 0), axis=1) - 1
    send_slots = send_slots.reshape(row_devices, capacity)
    got_rows, got_slots = (
        lax.all_to_all(send_rows, "row", split_axis=0, concat_axis=0, tiled=True),
        lax.all_to_all(send_slots, "row", split_axis=0, concat_axis=0, tiled=True),
    )
    got_rows = got_rows.reshape(row_devices * capacity, width)
    got_slots = got_slots.reshape(row_devices * capacity)
    slot_range = jnp.arange(slots_group, dtype=jnp.int32)
    piece_rows = lax.all_gather(got_rows, "col", axis=0, tiled=True)
    piece_slots = lax.all_gather(got_slots, "col", axis=0, tiled=True)
    safe_slots = jnp.where(piece_slots >= 0, piece_slots, slots_group).astype(jnp.int32)
    placed = (
        jnp.zeros((slots_group, width), jnp.bfloat16).at[safe_slots].set(piece_rows, mode="drop")
    )
    group_index = lax.axis_index("row")
    slot_pos = slot_range * row_devices + group_index
    in_task = (slot_pos[:, None] >= task_base[None, :]) & (
        slot_pos[:, None] < (task_base + totals)[None, :]
    )
    task_term = jnp.dot(
        in_task.astype(jnp.bfloat16), task_embed, preferred_element_type=jnp.float32
    )
    hidden = (placed.astype(jnp.float32) + task_term).astype(jnp.bfloat16)
    part_width = width // col_devices
    column = lax.axis_index("col") * part_width
    layers = layer_weight.shape[0]
    result = hidden
    for layer_index in range(layers):
        active = activate_rows(hidden, norm_gain[layer_index])
        update = jnp.dot(active, layer_weight[layer_index], preferred_element_type=jnp.float32)
        own_cols = lax.dynamic_slice_in_dim(hidden, column, part_width, 1).astype(jnp.float32)
        result = (own_cols + update).astype(jnp.bfloat16)
        if layer_index + 1 < layers:
            hidden = lax.all_gather(result, "col", axis=1, tiled=True)
    return result


def solution(mesh):
    return jax.shard_map(
        shards,
        mesh=mesh,
        in_specs=(P(("row", "col"), None), P(("row", "col")), P(), P(), P(None, None, "col")),
        out_specs=P("row", "col"),
        check_vma=False,
    )
```

profile of v0, /device:TPU:0, one launch (start us, length us, event | category | flops | bytes accessed | tf_op | source)
XLA Modules:
  0.0 303.9 jit_solution(6992512767991493794)
XLA Ops:
  6.5 0.0 copy-start
  6.5 0.0 copy-start.1
  6.5 0.0 all-gather.7.cloned.1.call-start
  6.5 0.8 convert_reduce_fusion.2
  7.4 0.9 convert_reduce_fusion.1
  8.3 0.7 broadcast_compare_fusion
  8.9 1.3 dynamic-slice.5
  10.9 0.2 dynamic-update-slice.1
  11.1 13.1 %all-reduce.3 = (s32[8]{0:T(128)S(1)}, s32[64]{0:T(128)S(1)}) all-reduce(s32[8]{0:T(128)S(1)} %convert_reduce_fusion.2, s32[64]{0:T(128)S(1)} %dynamic-update-slice.1), channel_id=1, replica_groups=mesh['row'=4,'col'=8] {'col'}, use_global_device_ids=true, to_apply=%region_1.2 | all-reduce | flops 72 | bytes 576 | tf_op jit(solution)/shard_map/psum | solution.py:51
  24.2 1.2 dynamic-slice.4
  26.1 0.2 dynamic-update-slice
  26.4 4.9 %all-reduce.4 = (s32[8]{0:T(128)S(1)}, s32[32]{0:T(128)S(1)}) all-reduce(s32[8]{0:T(128)S(1)} %get-tuple-element.117, s32[32]{0:T(128)S(1)} %dynamic-update-slice), channel_id=1, replica_groups=mesh['row'=4,'col'=8] {'row'}, use_global_device_ids=true, to_apply=%region_2.3 | all-reduce | flops 40 | bytes 320 | tf_op jit(solution)/shard_map/psum | solution.py:53
  31.3 0.1 reshape.226
  31.3 0.1 reshape.227
  31.4 0.2 reduce-window.8
  31.6 0.7 select_reduce_fusion.1
  32.4 0.2 convert_reduce_fusion
  32.6 0.7 add_select_fusion
  33.2 0.0 copy-done
  33.2 0.4 convolution_convert_fusion
  33.7 11.9 %all_to_all.11 = bf16[4,16,4096]{2,1,0:T(8,128)(2,1)} all-to-all(bf16[4,16,4096]{2,1,0:T(8,128)(2,1)S(1)} %bitcast.53), channel_id=1, replica_groups=mesh['row'=4,'col'=8] {'row'}, dimensions={0} | all-to-all | bytes 1048576 | tf_op jit(solution)/shard_map/all_to_all | solution.py:79
  45.6 0.0 all-gather.7.cloned.1.call-update
  45.6 0.1 select_reduce_fusion
  45.7 0.7 sub.18
  46.3 3.2 %all-to-all-start = ((s32[4,1,16]{2,1,0:T(1,128)}), s32[4,1,16]{2,1,0:T(1,128)S(1)}, u32[]{:S(2)}, u32[]{:S(2)}) async-start(s32[4,1,16]{2,1,0:T(1,128)} %bitcast.6), calls=%async_computation | async-start | bytes 4096 | tf_op jit(solution)/shard_map/all_to_all | solution.py:80
  49.6 0.0 all-gather.9.cloned.1.call-start
  50.3 1.1 fusion.112
  51.3 1.9 all-to-all-done
  53.2 0.5 broadcast.253
  53.8 0.7 reduce.3
  54.4 0.1 reshape.235
  54.5 0.2 dynamic-update-slice.2
  54.7 9.3 %all-reduce.2 = s32[512]{0:T(512)S(1)} all-reduce(s32[512]{0:T(512)S(1)} %dynamic-update-slice.2), channel_id=1, replica_groups=mesh['row'=4,'col'=8] {'col'}, use_global_device_ids=true, to_apply=%add.2 | all-reduce | flops 512 | bytes 4096
  64.0 52.0 %all-gather.7.cloned.1.call-done = bf16[512,4096]{1,0:T(8,128)(2,1)} async-done(((bf16[64,4096]{1,0:T(8,128)(2,1)}), bf16[512,4096]{1,0:T(8,128)(2,1)}) %all-gather.7.cloned.1.call-update) | async-done | bytes 4194320 | tf_op jit(solution)/shard_map/all_gather | solution.py:85
  116.0 8.2 %scatter_custom_fusion = bf16[256,4096]{1,0:T(8,128)(2,1)S(1)} fusion(s32[512]{0:T(512)S(1)} %compare_select_fusion, bf16[512,4096]{1,0:T(8,128)(2,1)} %all-gather.7.cloned.1.call-done, bf16[]{:T(256)} %constant.131.clone.1), kind=kCustom, calls=%fused_computation.74 | custom fusion | bytes 2097664 | tf_op jit(solution)/shard_map/scatter | solution.py:89
  124.3 0.0 copy-done.1
  124.3 1.0 fusion.1
  125.3 4.4 %fusion.92 = bf16[256,512]{1,0:T(8,128)(2,1)} fusion(bf16[4,4096,512]{2,1,0:T(8,128)(2,1)} %param.13, bf16[256,4096]{1,0:T(8,128)(2,1)S(1)} %get-tuple-element.130, f32[4096]{0:T(1024)S(1)} %bitcast.57, f32[256]{0:T(256)S(1)} %add_rsqrt_fusion.3, s32[]{:T(128)S(6)} %select_n.59), kind=kOutput, calls=%fused_computation.73 | convolution fusion | flops 1082523648 | bytes 6833156 | tf_op jit(solution)/shard_map/dot_general | solution.py:106
  129.7 0.0 all-gather.9.cloned.1.call-update
  129.7 0.2 all-gather.11.cloned.1.call-start
  129.9 48.8 %all-gather.9.cloned.1.call-done = bf16[256,4096]{1,0:T(8,128)(2,1)} async-done(((bf16[256,512]{1,0:T(8,128)(2,1)}), bf16[256,4096]{1,0:T(8,128)(2,1)}) %all-gather.9.cloned.1.call-update) | async-done | bytes 2097168 | tf_op jit(solution)/shard_map/all_gather | solution.py:110
  178.7 2.1 fusion.9
  180.8 5.0 %fusion.87 = bf16[256,512]{1,0:T(8,128)(2,1)} fusion(bf16[4,4096,512]{2,1,0:T(8,128)(2,1)} %param.13, bf16[256,4096]{1,0:T(8,128)(2,1)} %all-gather.9.cloned.1.call-done, f32[4096]{0:T(1024)S(1)} %bitcast.56, f32[256]{0:T(256)S(1)} %add_rsqrt_fusion.2, s32[]{:T(128)S(6)} %select_n.59), kind=kOutput, calls=%fused_computation.72 | convolution fusion | flops 1082523648 | bytes 6833156 | tf_op jit(solution)/shard_map/dot_general | solution.py:106
  185.8 0.0 all-gather.11.cloned.1.call-update
  185.8 0.0 all-gather.13.cloned.1.call-start
  185.8 48.6 %all-gather.11.cloned.1.call-done = bf16[256,4096]{1,0:T(8,128)(2,1)} async-done(((bf16[256,512]{1,0:T(8,128)(2,1)}), bf16[256,4096]{1,0:T(8,128)(2,1)}) %all-gather.11.cloned.1.call-update) | async-done | bytes 2097168 | tf_op jit(solution)/shard_map/all_gather | solution.py:110
  234.5 2.1 fusion.17
  236.6 5.0 %fusion.82 = bf16[256,512]{1,0:T(8,128)(2,1)} fusion(bf16[4,4096,512]{2,1,0:T(8,128)(2,1)} %param.13, bf16[256,4096]{1,0:T(8,128)(2,1)} %all-gather.11.cloned.1.call-done, f32[4096]{0:T(1024)S(1)} %bitcast.55, f32[256]{0:T(256)S(1)} %add_rsqrt_fusion.1, s32[]{:T(128)S(6)} %select_n.59), kind=kOutput, calls=%fused_computation.71 | convolution fusion | flops 1082523648 | bytes 6833156 | tf_op jit(solution)/shard_map/dot_general | solution.py:106
  241.5 0.0 all-gather.13.cloned.1.call-update
  241.6 48.8 %all-gather.13.cloned.1.call-done = bf16[256,4096]{1,0:T(8,128)(2,1)} async-done(((bf16[256,512]{1,0:T(8,128)(2,1)}), bf16[256,4096]{1,0:T(8,128)(2,1)}) %all-gather.13.cloned.1.call-update) | async-done | bytes 2097168 | tf_op jit(solution)/shard_map/all_gather | solution.py:110
  290.3 2.1 fusion.25
  292.4 5.0 %fusion.77 = bf16[256,512]{1,0:T(8,128)(2,1)} fusion(bf16[4,4096,512]{2,1,0:T(8,128)(2,1)} %param.13, bf16[256,4096]{1,0:T(8,128)(2,1)} %all-gather.13.cloned.1.call-done, f32[4096]{0:T(1024)S(1)} %bitcast.54, f32[256]{0:T(256)S(1)} %add_rsqrt_fusion, s32[]{:T(128)S(6)} %select_n.59), kind=kOutput, calls=%fused_computation.70 | convolution fusion | flops 1082523648 | bytes 6833156 | tf_op jit(solution)/shard_map/dot_general | solution.py:106
  (16 shorter events, 0.1 us)
Async XLA Ops:
  6.5 26.7 %copy-start = (bf16[32,4096]{1,0:T(8,128)(2,1)S(1)}, bf16[32,4096]{1,0:T(8,128)(2,1)}, u32[]{:S(2)}) copy-start(bf16[32,4096]{1,0:T(8,128)(2,1)} %param.9) | copy-start | bytes 786436
  6.5 117.7 %copy-start.1 = (bf16[8,4096]{1,0:T(8,128)(2,1)S(1)}, bf16[8,4096]{1,0:T(8,128)(2,1)}, u32[]{:S(2)}) copy-start(bf16[8,4096]{1,0:T(8,128)(2,1)} %param.11) | copy-start | bytes 196612
  6.5 109.5 %all-gather.7.cloned.1.call-start = ((), (), s32[]{:S(2)}) async-start(), calls=%async_computation.2 | async-start | bytes 4718592 | tf_op jit(solution)/shard_map/all_gather | solution.py:85
  46.3 6.9 %all-to-all-start = ((s32[4,1,16]{2,1,0:T(1,128)}), s32[4,1,16]{2,1,0:T(1,128)S(1)}, u32[]{:S(2)}, u32[]{:S(2)}) async-start(s32[4,1,16]{2,1,0:T(1,128)} %bitcast.6), calls=%async_computation | async-start | bytes 4096 | tf_op jit(solution)/shard_map/all_to_all | solution.py:80
  49.6 129.1 %all-gather.9.cloned.1.call-start = ((), (), s32[]{:S(2)}) async-start(), calls=%async_computation.3 | async-start | bytes 2359296 | tf_op jit(solution)/shard_map/all_gather | solution.py:110
  129.7 104.8 %all-gather.11.cloned.1.call-start = ((), (), s32[]{:S(2)}) async-start(), calls=%async_computation.4 | async-start | bytes 2359296 | tf_op jit(solution)/shard_map/all_gather | solution.py:110
  185.8 104.5 %all-gather.13.cloned.1.call-start = ((), (), s32[]{:S(2)}) async-start(), calls=%async_computation.5 | async-start | bytes 2359296 | tf_op jit(solution)/shard_map/all_gather | solution.py:110
Sparse Core Ops, SparseCore 0:
  45.7 70.2 all-gather.6
  129.8 48.8 all-gather.8
  185.9 48.5 all-gather.10
  241.7 48.5 all-gather.12
where the time goes:
time: 304 us
  waiting for transfers between devices  200 us (66%)
  blocking collectives  39.2 us (13%)
  matrix products  20.7 us (7%)
  between operations  15.1 us (5%)
  local copies, waits for them, and re-layouts  13.9 us (5%)
  other arithmetic  11.3 us (4%)
  starting transfers between devices  3.53 us (1%)
    all_gather x3, waiting for transfers between devices, shards(): hidden = lax.all_gather(result, 'col', axis=1, tiled=True)  146 us
    all_gather x1, waiting for transfers between devices, shards(): piece_rows = lax.all_gather(got_rows, 'col', axis=0, tiled=True)  52 us
    dot_general x4, matrix products, shards(): jnp.dot(active, layer_weight[layer_index], preferred_element_type=jnp.flo...  19.3 us
    psum x1, blocking collectives, shards(): row_total = lax.psum(counts, 'col')  13.1 us
    all_to_all x1, blocking collectives, shards(): lax.all_to_all(send_rows, 'row', split_axis=0, concat_axis=0, tiled=True)  11.9 us
    unnamed x1, blocking collectives  9.34 us
    scatter x1, local copies, waits for them, and re-layouts, shards(): jnp.zeros((slots_group, width), jnp.bfloat16).at[safe_slots]  8.22 us
    reduce_sum x3, other arithmetic, one_block(): jnp.mean(values * values, axis=1, keepdims=True) + epsilon  6.25 us
  transfers between devices with their start and end apart: 5, of which 5 were waited for; matrix products, arithmetic and copies ran while one was open for 1% of the time, Pallas kernels for 0%

commit v1 on v0

--- a/solution.py
+++ b/solution.py
@@ -82,7 +82,9 @@
     got_rows = got_rows.reshape(row_devices * capacity, width)
     got_slots = got_slots.reshape(row_devices * capacity)
     slot_range = jnp.arange(slots_group, dtype=jnp.int32)
-    piece_rows = lax.all_gather(got_rows, "col", axis=0, tiled=True)
+    piece_rows = jnp.concatenate(
+        lax.all_to_all(jnp.stack([got_rows] * lax.axis_size("col")), "col", 0, 0), axis=0
+    )
     piece_slots = lax.all_gather(got_slots, "col", axis=0, tiled=True)
     safe_slots = jnp.where(piece_slots >= 0, piece_slots, slots_group).astype(jnp.int32)
     placed = (

time: 304 us -> 341 us (1.12)
  blocking collectives: 39.2 us -> 120 us
  waiting for transfers between devices: 200 us -> 149 us
  starting transfers between devices: 3.53 us -> 8.2 us
    unnamed x1, blocking collectives: 9.34 us -> 91 us
    all_gather x1 -> x0, waiting for transfers between devices: 52 us -> none  [shards(): piece_rows = lax.all_gather(got_rows, 'col', axis=0, tiled=True)]
    all_to_all x0 -> x1, starting transfers between devices: none -> 4.68 us  [shards(): lax.all_to_all(jnp.stack([got_rows] * lax.axis_size('col')), 'col', 0, 0)]
  transfers between devices with their start and end apart: 5 -> 5, of which waited for: 5 -> 4; matrix products, arithmetic and copies ran while one was open for 1% -> 1% of each run, Pallas kernels for 0% -> 0%
where the time goes in v1:
time: 341 us; the launch traced here: 340 us
  waiting for transfers between devices  149 us (44%)
  blocking collectives  120 us (35%)
  matrix products  20.6 us (6%)
  local copies, waits for them, and re-layouts  15.4 us (5%)
  between operations  15.1 us (4%)
  other arithmetic  11.2 us (3%)
  starting transfers between devices  8.2 us (2%)
    all_gather x3, waiting for transfers between devices, shards(): hidden = lax.all_gather(result, 'col', axis=1, tiled=True)  146 us
    unnamed x1, blocking collectives  91 us
    dot_general x4, matrix products, shards(): jnp.dot(active, layer_weight[layer_index], preferred_element_type=jnp.flo...  19.2 us
    psum x1, blocking collectives, shards(): row_total = lax.psum(counts, 'col')  13.1 us
    all_to_all x1, blocking collectives, shards(): lax.all_to_all(send_rows, 'row', split_axis=0, concat_axis=0, tiled=True)  11.2 us
    scatter x1, local copies, waits for them, and re-layouts, shards(): jnp.zeros((slots_group, width), jnp.bfloat16).at[safe_slots]  8.22 us
  transfers between devices with their start and end apart: 5, of which 4 were waited for; matrix products, arithmetic and copies ran while one was open for 1% of the time, Pallas kernels for 0%

profile of v1, /device:TPU:0, one launch (start us, length us, event | category | flops | bytes accessed | tf_op | source)
XLA Modules:
  0.0 340.1 jit_solution(14075383895532243169)
XLA Ops:
  6.5 0.0 copy-start
  6.5 0.8 convert_reduce_fusion.2
  7.4 0.9 convert_reduce_fusion.1
  8.3 0.7 broadcast_compare_fusion
  8.9 1.2 dynamic-slice.5
  10.8 0.2 dynamic-update-slice.1
  11.1 13.1 %all-reduce.3 = (s32[8]{0:T(128)S(1)}, s32[64]{0:T(128)S(1)}) all-reduce(s32[8]{0:T(128)S(1)} %convert_reduce_fusion.2, s32[64]{0:T(128)S(1)} %dynamic-update-slice.1), channel_id=1, replica_groups=mesh['row'=4,'col'=8] {'col'}, use_global_device_ids=true, to_apply=%region_1.2 | all-reduce | flops 72 | bytes 576 | tf_op jit(solution)/shard_map/psum | solution.py:51
  24.1 1.2 dynamic-slice.4
  26.0 0.2 dynamic-update-slice
  26.3 4.9 %all-reduce.4 = (s32[8]{0:T(128)S(1)}, s32[32]{0:T(128)S(1)}) all-reduce(s32[8]{0:T(128)S(1)} %get-tuple-element.117, s32[32]{0:T(128)S(1)} %dynamic-update-slice), channel_id=1, replica_groups=mesh['row'=4,'col'=8] {'row'}, use_global_device_ids=true, to_apply=%region_2.3 | all-reduce | flops 40 | bytes 320 | tf_op jit(solution)/shard_map/psum | solution.py:53
  31.2 0.1 reshape.228
  31.3 0.1 reshape.229
  31.4 0.2 reduce-window.8
  31.6 0.7 select_reduce_fusion.1
  32.3 0.2 convert_reduce_fusion
  32.5 0.7 add_select_fusion
  33.2 0.1 select_reduce_fusion
  33.3 0.7 sub.18
  33.9 3.2 all-to-all-start
  37.2 0.0 copy-done
  37.2 0.4 convolution_convert_fusion
  37.6 3.2 all-to-all-done
  40.8 11.2 %all_to_all.16 = bf16[4,16,4096]{2,1,0:T(8,128)(2,1)S(1)} all-to-all(bf16[4,16,4096]{2,1,0:T(8,128)(2,1)S(1)} %bitcast.54), channel_id=1, replica_groups=mesh['row'=4,'col'=8] {'row'}, dimensions={0} | all-to-all | bytes 1048576 | tf_op jit(solution)/shard_map/all_to_all | solution.py:79
  52.0 2.5 stack.3
  54.5 0.0 copy-start.1
  54.5 0.0 copy-start.2
  54.5 4.7 %all-to-all-start.2 = ((bf16[8,64,4096]{2,1,0:T(8,128)(2,1)}), bf16[8,64,4096]{2,1,0:T(8,128)(2,1)}, u32[]{:S(2)}, u32[]{:S(2)}) async-start(bf16[8,64,4096]{2,1,0:T(8,128)(2,1)} %stack.3), calls=%async_computation.2 | async-start | bytes 8388608 | tf_op jit(solution)/shard_map/all_to_all | solution.py:86
  59.2 0.0 all-gather.6.cloned.1.call-start
  59.9 0.0 copy-done.1
  60.0 0.5 broadcast.254
  60.5 0.7 reduce.3
  61.2 0.1 reshape.237
  61.2 0.2 dynamic-update-slice.2
  61.4 91.0 %all-reduce.2 = s32[512]{0:T(512)S(1)} all-reduce(s32[512]{0:T(512)S(1)} %dynamic-update-slice.2), channel_id=1, replica_groups=mesh['row'=4,'col'=8] {'col'}, use_global_device_ids=true, to_apply=%add.2 | all-reduce | flops 512 | bytes 4096
  152.5 0.0 all-to-all-done.2
  152.5 8.2 %scatter_custom_fusion = bf16[256,4096]{1,0:T(8,128)(2,1)S(1)} fusion(s32[512]{0:T(512)S(1)} %compare_select_fusion, bf16[512,4096]{1,0:T(8,128)(2,1)} %bitcast.10, bf16[]{:T(256)} %constant.131.clone.1), kind=kCustom, calls=%fused_computation.74 | custom fusion | bytes 2097664 | tf_op jit(solution)/shard_map/scatter | solution.py:91
  160.7 0.0 copy-done.2
  160.7 1.0 fusion.1
  161.7 4.3 %fusion.92 = bf16[256,512]{1,0:T(8,128)(2,1)} fusion(bf16[4,4096,512]{2,1,0:T(8,128)(2,1)} %param.13, bf16[256,4096]{1,0:T(8,128)(2,1)S(1)} %get-tuple-element.130, f32[4096]{0:T(1024)S(1)} %bitcast.58, f32[256]{0:T(256)S(1)} %add_rsqrt_fusion.3, s32[]{:T(128)S(6)} %select_n.59), kind=kOutput, calls=%fused_computation.73 | convolution fusion | flops 1082523648 | bytes 6833156 | tf_op jit(solution)/shard_map/dot_general | solution.py:108
  166.0 0.0 all-gather.6.cloned.1.call-update
  166.0 0.2 all-gather.8.cloned.1.call-start
  166.3 48.6 %all-gather.6.cloned.1.call-done = bf16[256,4096]{1,0:T(8,128)(2,1)} async-done(((bf16[256,512]{1,0:T(8,128)(2,1)}), bf16[256,4096]{1,0:T(8,128)(2,1)}) %all-gather.6.cloned.1.call-update) | async-done | bytes 2097168 | tf_op jit(solution)/shard_map/all_gather | solution.py:112
  214.9 2.1 fusion.9
  217.0 5.0 %fusion.87 = bf16[256,512]{1,0:T(8,128)(2,1)} fusion(bf16[4,4096,512]{2,1,0:T(8,128)(2,1)} %param.13, bf16[256,4096]{1,0:T(8,128)(2,1)} %all-gather.6.cloned.1.call-done, f32[4096]{0:T(1024)S(1)} %bitcast.57, f32[256]{0:T(256)S(1)} %add_rsqrt_fusion.2, s32[]{:T(128)S(6)} %select_n.59), kind=kOutput, calls=%fused_computation.72 | convolution fusion | flops 1082523648 | bytes 6833156 | tf_op jit(solution)/shard_map/dot_general | solution.py:108
  222.0 0.0 all-gather.8.cloned.1.call-update
  222.0 0.0 all-gather.10.cloned.1.call-start
  222.0 48.6 %all-gather.8.cloned.1.call-done = bf16[256,4096]{1,0:T(8,128)(2,1)} async-done(((bf16[256,512]{1,0:T(8,128)(2,1)}), bf16[256,4096]{1,0:T(8,128)(2,1)}) %all-gather.8.cloned.1.call-update) | async-done | bytes 2097168 | tf_op jit(solution)/shard_map/all_gather | solution.py:112
  270.7 2.1 fusion.17
  272.8 5.0 %fusion.82 = bf16[256,512]{1,0:T(8,128)(2,1)} fusion(bf16[4,4096,512]{2,1,0:T(8,128)(2,1)} %param.13, bf16[256,4096]{1,0:T(8,128)(2,1)} %all-gather.8.cloned.1.call-done, f32[4096]{0:T(1024)S(1)} %bitcast.56, f32[256]{0:T(256)S(1)} %add_rsqrt_fusion.1, s32[]{:T(128)S(6)} %select_n.59), kind=kOutput, calls=%fused_computation.71 | convolution fusion | flops 1082523648 | bytes 6833156 | tf_op jit(solution)/shard_map/dot_general | solution.py:108
  277.7 0.0 all-gather.10.cloned.1.call-update
  277.8 48.8 %all-gather.10.cloned.1.call-done = bf16[256,4096]{1,0:T(8,128)(2,1)} async-done(((bf16[256,512]{1,0:T(8,128)(2,1)}), bf16[256,4096]{1,0:T(8,128)(2,1)}) %all-gather.10.cloned.1.call-update) | async-done | bytes 2097168 | tf_op jit(solution)/shard_map/all_gather | solution.py:112
  326.5 2.1 fusion.25
  328.6 5.0 %fusion.77 = bf16[256,512]{1,0:T(8,128)(2,1)} fusion(bf16[4,4096,512]{2,1,0:T(8,128)(2,1)} %param.13, bf16[256,4096]{1,0:T(8,128)(2,1)} %all-gather.10.cloned.1.call-done, f32[4096]{0:T(1024)S(1)} %bitcast.55, f32[256]{0:T(256)S(1)} %add_rsqrt_fusion, s32[]{:T(128)S(6)} %select_n.59), kind=kOutput, calls=%fused_computation.70 | convolution fusion | flops 1082523648 | bytes 6833156 | tf_op jit(solution)/shard_map/dot_general | solution.py:108
  (17 shorter events, 0.1 us)
Async XLA Ops:
  6.5 30.6 %copy-start = (bf16[32,4096]{1,0:T(8,128)(2,1)S(1)}, bf16[32,4096]{1,0:T(8,128)(2,1)}, u32[]{:S(2)}) copy-start(bf16[32,4096]{1,0:T(8,128)(2,1)} %param.9) | copy-start | bytes 786436
  33.9 6.9 %all-to-all-start = ((s32[4,1,16]{2,1,0:T(1,128)}), s32[4,1,16]{2,1,0:T(1,128)S(1)}, u32[]{:S(2)}, u32[]{:S(2)}) async-start(s32[4,1,16]{2,1,0:T(1,128)} %bitcast.6), calls=%async_computation | async-start | bytes 4096 | tf_op jit(solution)/shard_map/all_to_all | solution.py:80
  54.5 5.4 %copy-start.1 = (f32[4,4096]{1,0:T(4,128)S(1)}, f32[4,4096]{1,0:T(4,128)}, u32[]{:S(2)}) copy-start(f32[4,4096]{1,0:T(4,128)} %param.12) | copy-start | bytes 196612
  54.5 106.2 %copy-start.2 = (bf16[8,4096]{1,0:T(8,128)(2,1)S(1)}, bf16[8,4096]{1,0:T(8,128)(2,1)}, u32[]{:S(2)}) copy-start(bf16[8,4096]{1,0:T(8,128)(2,1)} %param.11) | copy-start | bytes 196612
  54.5 97.9 %all-to-all-start.2 = ((bf16[8,64,4096]{2,1,0:T(8,128)(2,1)}), bf16[8,64,4096]{2,1,0:T(8,128)(2,1)}, u32[]{:S(2)}, u32[]{:S(2)}) async-start(bf16[8,64,4096]{2,1,0:T(8,128)(2,1)} %stack.3), calls=%async_computation.2 | async-start | bytes 8388608 | tf_op jit(solution)/shard_map/all_to_all | solution.py:86
  59.2 155.7 %all-gather.6.cloned.1.call-start = ((), (), s32[]{:S(2)}) async-start(), calls=%async_computation.3 | async-start | bytes 2359296 | tf_op jit(solution)/shard_map/all_gather | solution.py:112
  166.0 104.6 %all-gather.8.cloned.1.call-start = ((), (), s32[]{:S(2)}) async-start(), calls=%async_computation.4 | async-start | bytes 2359296 | tf_op jit(solution)/shard_map/all_gather | solution.py:112
  222.0 104.5 %all-gather.10.cloned.1.call-start = ((), (), s32[]{:S(2)}) async-start(), calls=%async_computation.5 | async-start | bytes 2359296 | tf_op jit(solution)/shard_map/all_gather | solution.py:112
Sparse Core Ops, SparseCore 0:
  166.2 48.6 all-gather.5
  222.1 48.5 all-gather.7
  277.9 48.5 all-gather.9
